TPU v7x, 32 devices: a whole 2x2x4 slice. The times are simulated.
32 devices in a mesh: grp: 2 (over y), zt: 4 (over x, core), xy: 4 (over z).
Axes of the slice: x: 2, y: 2, z: 4, core: 2. Of those that a mesh axis runs over, the one named last changes fastest.
Arguments:
- source: float32 [2, 2, 3, 8, 16, 128], P('grp', None, None, 'xy', 'zt'), may hold values from -6 to 6
- links: float32 [4, 2, 3, 3, 8, 16, 128], P('grp', None, None, None, 'xy', 'zt'), may hold values from -2 to 2
- shifts: float32 [12], replicated, may hold values from 0.01 to 0.5
- residues: float32 [12], replicated, may hold values from 0.05 to 0.5
- mass: float32 [1], replicated, may hold values from 0.1 to 0.5
Outputs:
- rational: float32 [2, 2, 3, 8, 16, 128], P('grp', None, None, 'xy', 'zt')
- action: float32 [1], replicated
All inputs are finite; a program needn't handle non-finite values.
Results may differ from a plain program's by a relative error of at most 0.0003.
Values sent between devices are 32-bit elements; how exact they have to be, the bound alone decides.
A program may use at most 64 MiB of HBM per device.

v0:
```python
import jax
import jax.numpy as jnp
from jax import lax
from jax.sharding import PartitionSpec as P

NY = 2
NZ = 64
ITERS = 8


def shifted(block, axis, distance):
    devices = range(lax.axis_size(axis))
    route = [((i - distance) % len(devices), i) for i in devices]
    return lax.ppermute(block, axis, route)


def extended(block, sides, width):
    for axis, dim in sides:
        count = lax.axis_size(axis)
        forward = [(i, i + 1) for i in range(count - 1)]
        forward.append((count - 1, 0))
        backward = [(target, source) for source, target in forward]
        low = lax.ppermute(
            lax.slice_in_dim(block, block.shape[dim] - width, None, axis=dim), axis, forward
        )
        high = lax.ppermute(lax.slice_in_dim(block, 0, width, axis=dim), axis, backward)
        block = jnp.concatenate([low, block, high], axis=dim)
    return block


def sign_of(values):
    return (1 - 2 * (values % 2)).astype(jnp.float32)


def phases(coord_x, coord_t, last_t):
    yz_index = jnp.arange(NY * NZ, dtype=jnp.int32)
    ycoord = yz_index // NZ
    zcoord = yz_index % NZ
    unity = jnp.ones((coord_x.shape[0], coord_t.shape[0], NY * NZ), jnp.float32)
    boundary = jnp.where(coord_t == last_t, -1.0, 1.0).astype(jnp.float32)
    eta_y = sign_of(coord_x)[:, None, None] * unity
    eta_z = sign_of(coord_x[:, None, None] + ycoord[None, None, :]) * unity
    eta_t = (
        sign_of(coord_x[:, None, None] + ycoord[None, None, :] + zcoord[None, None, :])
        * boundary[None, :, None]
    )
    return jnp.stack([unity, eta_y, eta_z, eta_t])


def times_link(link, field):
    real = jnp.sum(
        link[0][None] * field[:, 0][:, None] - link[1][None] * field[:, 1][:, None], axis=2
    )
    imag = jnp.sum(
        link[0][None] * field[:, 1][:, None] + link[1][None] * field[:, 0][:, None], axis=2
    )
    return jnp.stack([real, imag], axis=1)


def times_adjoint(link, field):
    real = jnp.sum(
        link[0][None] * field[:, 0][:, :, None] + link[1][None] * field[:, 1][:, :, None], axis=1
    )
    imag = jnp.sum(
        link[0][None] * field[:, 1][:, :, None] - link[1][None] * field[:, 0][:, :, None], axis=1
    )
    return jnp.stack([real, imag], axis=1)


def roll_ycoord(values, offset):
    return jnp.roll(values, offset * NZ, axis=-1)


def roll_zcoord(values, offset):
    shape = values.shape
    return jnp.roll(values.reshape(shape[:-1] + (NY, NZ)), offset, axis=-1).reshape(shape)


def hopping(field, link):
    inner_field = field[..., 1:-1, 1:-1, :]
    inner_link = link[..., 1:-1, 1:-1, :]
    total = times_link(inner_link[0], field[..., 2:, 1:-1, :]) - times_adjoint(
        link[0][..., :-2, 1:-1, :], field[..., :-2, 1:-1, :]
    )
    total = (
        total
        + times_link(inner_link[1], roll_ycoord(inner_field, -1))
        - roll_ycoord(times_adjoint(inner_link[1], inner_field), 1)
    )
    total = (
        total
        + times_link(inner_link[2], roll_zcoord(inner_field, -1))
        - roll_zcoord(times_adjoint(inner_link[2], inner_field), 1)
    )
    total = (
        total
        + times_link(inner_link[3], field[..., 1:-1, 2:, :])
        - times_adjoint(link[3][..., 1:-1, :-2, :], field[..., 1:-1, :-2, :])
    )
    return 0.5 * total


def local_dot(left, right):
    return jnp.sum(left * right, axis=(1, 2, 3, 4, 5))


def spread(values):
    return values.reshape(values.shape + (1, 1, 1, 1, 1))


def on_device(source, links, shifts, residues, mass):
    all_links = lax.all_gather(links, "grp", axis=0, tiled=True)
    cells_x = source.shape[3]
    cells_t = source.shape[4]
    coord_x = lax.axis_index("xy") * cells_x + jnp.arange(cells_x, dtype=jnp.int32)
    coord_t = lax.axis_index("zt") * cells_t + jnp.arange(cells_t, dtype=jnp.int32)
    eta = phases(coord_x, coord_t, cells_t * lax.axis_size("zt") - 1)
    folded = all_links * eta[:, None, None, None]
    mass_sq = mass[0] * mass[0]
    rim_x = shifted(folded[0][:, :, :, -1:, :, :], "xy", 1)
    rim_t = shifted(folded[3][:, :, :, :, -1:, :], "zt", 1)
    wide_links = jnp.pad(folded, ((0, 0), (0, 0), (0, 0), (0, 0), (1, 1), (1, 1), (0, 0)))
    wide_links = wide_links.at[0, :, :, :, 0:1, 1:-1, :].set(rim_x)
    wide_links = wide_links.at[3, :, :, :, 1:-1, 0:1, :].set(rim_t)

    def with_faces(field):
        return extended(field, (("zt", 4), ("xy", 3)), 1)

    shift_col = shifts[:, None]
    members = source.shape[0]
    residual = source
    direction = source
    solutions = jnp.zeros((shifts.shape[0],) + source.shape, jnp.float32)
    directions = jnp.broadcast_to(source[None], solutions.shape)
    norm_now = lax.psum(local_dot(source, source), ("zt", "xy"))
    zeta_now = jnp.ones((shifts.shape[0], members), jnp.float32)
    zeta_old = jnp.ones((shifts.shape[0], members), jnp.float32)
    alpha_old = jnp.ones((members,), jnp.float32)
    beta_old = jnp.zeros((members,), jnp.float32)
    for iteration in range(ITERS):
        first_hop = hopping(with_faces(direction), wide_links)
        image = mass_sq * direction - hopping(with_faces(first_hop), wide_links)
        curvature_sum, cross_sum, image_sum = lax.psum(
            (local_dot(direction, image), local_dot(residual, image), local_dot(image, image)),
            ("zt", "xy"),
        )
        alpha_now = norm_now / curvature_sum
        zeta_new = (
            zeta_now
            * zeta_old
            * alpha_old
            / (
                alpha_now * beta_old * (zeta_old - zeta_now)
                + zeta_old * alpha_old * (1.0 + shift_col * alpha_now)
            )
        )
        alpha_shift = alpha_now * zeta_new / zeta_now
        solutions = solutions + spread(alpha_shift) * directions
        if iteration + 1 < ITERS:
            residual = residual - spread(alpha_now) * image
            norm_next = norm_now - 2.0 * alpha_now * cross_sum + alpha_now * alpha_now * image_sum
            beta_now = norm_next / norm_now
            beta_shift = beta_now * (zeta_new / zeta_now) ** 2
            direction = residual + spread(beta_now) * direction
            directions = spread(zeta_new) * residual[None] + spread(beta_shift) * directions
            zeta_old = zeta_now
            zeta_now = zeta_new
            alpha_old = alpha_now
            beta_old = beta_now
            norm_now = norm_next
    rational = jnp.sum(residues.reshape((-1, 1, 1, 1, 1, 1, 1)) * solutions, axis=0)
    total = lax.psum(jnp.sum(source * rational), ("grp", "zt", "xy"))
    site_count = (
        members
        * lax.axis_size("grp")
        * cells_x
        * lax.axis_size("xy")
        * cells_t
        * lax.axis_size("zt")
        * NY
        * NZ
    )
    action = (total / site_count).reshape(1)
    return (rational, action)


def solution(mesh):
    placed = (
        P("grp", None, None, "xy", "zt", None),
        P("grp", None, None, None, "xy", "zt", None),
        P(),
        P(),
        P(),
    )
    return jax.shard_map(
        on_device,
        mesh=mesh,
        in_specs=placed,
        out_specs=(P("grp", None, None, "xy", "zt", None), P()),
        check_vma=False,
    )
```

profile of v0, /device:TPU:0, one launch (start us, length us, event | category | flops | bytes accessed | tf_op | source)
XLA Modules:
  0.0 512.2 jit_solution(10780419264730769000)
XLA Ops:
  0.7 7.8 %all_gather.3 = f32[4,2,3,3,2,4,128]{6,5,4,3,2,1,0:T(4,128)S(1)} all-gather(f32[2,2,3,3,2,4,128]{6,5,4,3,2,1,0:T(4,128)} %param.10), channel_id=1, replica_groups=mesh['grp'=2,'zt'=4,'xy'=4] {'grp'}, dimensions={0}, use_global_device_ids=true | all-gather | bytes 442368 | tf_op jit(solution)/shard_map/all_gather | solution.py:112
  18.0 3.9 collective-permute-done.5
  31.7 2.6 collective-permute-done.9
  36.1 30.7 %all-reduce.7 = (f32[1]{0:T(128)}, f32[1]{0:T(128)}, f32[1]{0:T(128)}) all-reduce(f32[1]{0:T(128)} %bitcast, f32[1]{0:T(128)} %bitcast.76, f32[1]{0:T(128)} %bitcast.80), channel_id=1, replica_groups=mesh['grp'=2,'zt'=4,'xy'=4] {'zt','xy'}, use_global_device_ids=true, to_apply=%region_1.2 | all-reduce | flops 3 | bytes 24 | tf_op jit(solution)/shard_map/psum | solution.py:135
  78.4 3.0 collective-permute-done.13
  91.1 2.3 collective-permute-done.17
  95.2 30.6 %all-reduce.6 = (f32[1]{0:T(128)}, f32[1]{0:T(128)}, f32[1]{0:T(128)}) all-reduce(f32[1]{0:T(128)} %bitcast.140, f32[1]{0:T(128)} %bitcast.144, f32[1]{0:T(128)} %bitcast.145), channel_id=1, replica_groups=mesh['grp'=2,'zt'=4,'xy'=4] {'zt','xy'}, use_global_device_ids=true, to_apply=%region_71.72 | all-reduce | flops 3 | bytes 24 | tf_op jit(solution)/shard_map/psum | solution.py:143
  135.4 2.8 collective-permute-done.21
  147.7 2.5 collective-permute-done.25
  152.0 30.4 %all-reduce.5 = (f32[1]{0:T(128)}, f32[1]{0:T(128)}, f32[1]{0:T(128)}) all-reduce(f32[1]{0:T(128)} %bitcast.205, f32[1]{0:T(128)} %bitcast.209, f32[1]{0:T(128)} %bitcast.210), channel_id=1, replica_groups=mesh['grp'=2,'zt'=4,'xy'=4] {'zt','xy'}, use_global_device_ids=true, to_apply=%region_109.110 | all-reduce | flops 3 | bytes 24 | tf_op jit(solution)/shard_map/psum | solution.py:143
  192.2 3.1 collective-permute-done.29
  205.0 2.3 collective-permute-done.33
  209.2 30.6 %all-reduce.4 = (f32[1]{0:T(128)}, f32[1]{0:T(128)}, f32[1]{0:T(128)}) all-reduce(f32[1]{0:T(128)} %bitcast.270, f32[1]{0:T(128)} %bitcast.274, f32[1]{0:T(128)} %bitcast.275), channel_id=1, replica_groups=mesh['grp'=2,'zt'=4,'xy'=4] {'zt','xy'}, use_global_device_ids=true, to_apply=%region_147.148 | all-reduce | flops 3 | bytes 24 | tf_op jit(solution)/shard_map/psum | solution.py:143
  249.3 2.8 collective-permute-done.37
  261.7 2.5 collective-permute-done.41
  265.9 30.4 %all-reduce.3 = (f32[1]{0:T(128)}, f32[1]{0:T(128)}, f32[1]{0:T(128)}) all-reduce(f32[1]{0:T(128)} %bitcast.335, f32[1]{0:T(128)} %bitcast.339, f32[1]{0:T(128)} %bitcast.340), channel_id=1, replica_groups=mesh['grp'=2,'zt'=4,'xy'=4] {'zt','xy'}, use_global_device_ids=true, to_apply=%region_185.186 | all-reduce | flops 3 | bytes 24 | tf_op jit(solution)/shard_map/psum | solution.py:143
  306.2 3.1 collective-permute-done.45
  323.1 30.6 %all-reduce.2 = (f32[1]{0:T(128)}, f32[1]{0:T(128)}, f32[1]{0:T(128)}) all-reduce(f32[1]{0:T(128)} %bitcast.400, f32[1]{0:T(128)} %bitcast.404, f32[1]{0:T(128)} %bitcast.405), channel_id=1, replica_groups=mesh['grp'=2,'zt'=4,'xy'=4] {'zt','xy'}, use_global_device_ids=true, to_apply=%region_223.224 | all-reduce | flops 3 | bytes 24 | tf_op jit(solution)/shard_map/psum | solution.py:143
  363.4 2.8 collective-permute-done.53
  375.7 2.5 collective-permute-done.57
  380.0 30.4 %all-reduce.1 = (f32[1]{0:T(128)}, f32[1]{0:T(128)}, f32[1]{0:T(128)}) all-reduce(f32[1]{0:T(128)} %bitcast.465, f32[1]{0:T(128)} %bitcast.469, f32[1]{0:T(128)} %bitcast.470), channel_id=1, replica_groups=mesh['grp'=2,'zt'=4,'xy'=4] {'zt','xy'}, use_global_device_ids=true, to_apply=%region_261.262 | all-reduce | flops 3 | bytes 24 | tf_op jit(solution)/shard_map/psum | solution.py:143
  420.2 3.1 collective-permute-done.61
  437.0 30.6 %psum.185 = f32[1]{0:T(128)} all-reduce(f32[1]{0:T(128)} %bitcast.531), channel_id=1, replica_groups=mesh['grp'=2,'zt'=4,'xy'=4] {'zt','xy'}, use_global_device_ids=true, to_apply=%region_299.300 | all-reduce | flops 1 | bytes 8 | tf_op jit(solution)/shard_map/psum | solution.py:143
  469.9 40.5 %psum.186 = f32[]{:T(128)} all-reduce(f32[]{:T(128)} %multiply_reduce_fusion.1), channel_id=1, replica_groups=mesh['grp'=2,'zt'=4,'xy'=4] {'grp','zt','xy'}, use_global_device_ids=true, to_apply=%region_302.303 | all-reduce | flops 1 | bytes 8 | tf_op jit(solution)/shard_map/psum | solution.py:172
  (739 shorter events, 158.2 us)
Async XLA Ops:
  8.8 13.1 %collective-permute-start = (f32[2,3,3,1,4,128]{5,4,3,2,1,0:T(4,128)S(1)}, f32[2,3,3,1,4,128]{5,4,3,2,1,0:T(4,128)S(1)}, u32[]{:S(2)}, u32[]{:S(2)}) collective-permute-start(f32[2,3,3,1,4,128]{5,4,3,2,1,0:T(4,128)S(1)} %slice.3115), channel_id=1, source_target_pairs={{3,0},{0,1},{1,2},{2,3},{7,4},{4,5},{5,6},{6,7},{11,8},{8,9},{9,10... | collective-permute-start | bytes 110600 | tf_op jit(solution)/shard_map/ppermute | solution.py:14
  10.7 11.4 %collective-permute-start.1 = (f32[2,3,3,2,1,128]{5,4,3,2,1,0:T(1,128)S(1)}, f32[2,3,3,2,1,128]{5,4,3,2,1,0:T(1,128)S(1)}, u32[]{:S(2)}, u32[]{:S(2)}) collective-permute-start(f32[2,3,3,2,1,128]{5,4,3,2,1,0:T(1,128)S(1)} %slice.3117), channel_id=1, source_target_pairs={{12,0},{0,4},{4,8},{8,12},{13,1},{1,5},{5,9},{9,13},{14,2},{2,6},{... | collective-permute-start | bytes 55304 | tf_op jit(solution)/shard_map/ppermute | solution.py:14
  16.2 5.6 %collective-permute-start.5 = (f32[1,2,3,1,6,128]{5,4,3,2,1,0:T(8,128)S(1)}, f32[1,2,3,1,6,128]{5,4,3,2,1,0:T(8,128)S(1)}, u32[]{:S(2)}, u32[]{:S(2)}) collective-permute-start(f32[1,2,3,1,6,128]{5,4,3,2,1,0:T(8,128)S(1)} %get-tuple-element.617), channel_id=1, source_target_pairs={{0,1},{1,2},{2,3},{3,0},{4,5},{5,6},{6,7},{7,4},{8,9},{9,10},{10,1... | collective-permute-start | bytes 55304 | tf_op jit(solution)/shard_map/ppermute | solution.py:23
  28.6 5.8 %collective-permute-start.9 = (f32[1,2,3,1,6,128]{5,4,3,2,1,0:T(8,128)S(1)}, f32[1,2,3,1,6,128]{5,4,3,2,1,0:T(8,128)S(1)}, u32[]{:S(2)}, u32[]{:S(2)}) collective-permute-start(f32[1,2,3,1,6,128]{5,4,3,2,1,0:T(8,128)S(1)} %get-tuple-element.613), channel_id=1, source_target_pairs={{0,1},{1,2},{2,3},{3,0},{4,5},{5,6},{6,7},{7,4},{8,9},{9,10},{10,1... | collective-permute-start | bytes 55304 | tf_op jit(solution)/shard_map/ppermute | solution.py:23
  75.5 5.8 %collective-permute-start.13 = (f32[1,2,3,1,6,128]{5,4,3,2,1,0:T(8,128)S(1)}, f32[1,2,3,1,6,128]{5,4,3,2,1,0:T(8,128)S(1)}, u32[]{:S(2)}, u32[]{:S(2)}) collective-permute-start(f32[1,2,3,1,6,128]{5,4,3,2,1,0:T(8,128)S(1)} %get-tuple-element.609), channel_id=1, source_target_pairs={{0,1},{1,2},{2,3},{3,0},{4,5},{5,6},{6,7},{7,4},{8,9},{9,10},{10,1... | collective-permute-start | bytes 55304 | tf_op jit(solution)/shard_map/ppermute | solution.py:23
  87.0 4.1 collective-permute-start.16
  87.6 5.8 %collective-permute-start.17 = (f32[1,2,3,1,6,128]{5,4,3,2,1,0:T(8,128)S(1)}, f32[1,2,3,1,6,128]{5,4,3,2,1,0:T(8,128)S(1)}, u32[]{:S(2)}, u32[]{:S(2)}) collective-permute-start(f32[1,2,3,1,6,128]{5,4,3,2,1,0:T(8,128)S(1)} %get-tuple-element.605), channel_id=1, source_target_pairs={{0,1},{1,2},{2,3},{3,0},{4,5},{5,6},{6,7},{7,4},{8,9},{9,10},{10,1... | collective-permute-start | bytes 55304 | tf_op jit(solution)/shard_map/ppermute | solution.py:23
  132.5 5.6 %collective-permute-start.21 = (f32[1,2,3,1,6,128]{5,4,3,2,1,0:T(8,128)S(1)}, f32[1,2,3,1,6,128]{5,4,3,2,1,0:T(8,128)S(1)}, u32[]{:S(2)}, u32[]{:S(2)}) collective-permute-start(f32[1,2,3,1,6,128]{5,4,3,2,1,0:T(8,128)S(1)} %get-tuple-element.601), channel_id=1, source_target_pairs={{0,1},{1,2},{2,3},{3,0},{4,5},{5,6},{6,7},{7,4},{8,9},{9,10},{10,1... | collective-permute-start | bytes 55304 | tf_op jit(solution)/shard_map/ppermute | solution.py:23
  144.6 5.6 %collective-permute-start.25 = (f32[1,2,3,1,6,128]{5,4,3,2,1,0:T(8,128)S(1)}, f32[1,2,3,1,6,128]{5,4,3,2,1,0:T(8,128)S(1)}, u32[]{:S(2)}, u32[]{:S(2)}) collective-permute-start(f32[1,2,3,1,6,128]{5,4,3,2,1,0:T(8,128)S(1)} %get-tuple-element.597), channel_id=1, source_target_pairs={{0,1},{1,2},{2,3},{3,0},{4,5},{5,6},{6,7},{7,4},{8,9},{9,10},{10,1... | collective-permute-start | bytes 55304 | tf_op jit(solution)/shard_map/ppermute | solution.py:23
  188.2 4.1 collective-permute-start.28
  189.4 5.8 %collective-permute-start.29 = (f32[1,2,3,1,6,128]{5,4,3,2,1,0:T(8,128)S(1)}, f32[1,2,3,1,6,128]{5,4,3,2,1,0:T(8,128)S(1)}, u32[]{:S(2)}, u32[]{:S(2)}) collective-permute-start(f32[1,2,3,1,6,128]{5,4,3,2,1,0:T(8,128)S(1)} %get-tuple-element.593), channel_id=1, source_target_pairs={{0,1},{1,2},{2,3},{3,0},{4,5},{5,6},{6,7},{7,4},{8,9},{9,10},{10,1... | collective-permute-start | bytes 55304 | tf_op jit(solution)/shard_map/ppermute | solution.py:23
  200.9 4.1 collective-permute-start.32
  201.5 5.9 %collective-permute-start.33 = (f32[1,2,3,1,6,128]{5,4,3,2,1,0:T(8,128)S(1)}, f32[1,2,3,1,6,128]{5,4,3,2,1,0:T(8,128)S(1)}, u32[]{:S(2)}, u32[]{:S(2)}) collective-permute-start(f32[1,2,3,1,6,128]{5,4,3,2,1,0:T(8,128)S(1)} %get-tuple-element.589), channel_id=1, source_target_pairs={{0,1},{1,2},{2,3},{3,0},{4,5},{5,6},{6,7},{7,4},{8,9},{9,10},{10,1... | collective-permute-start | bytes 55304 | tf_op jit(solution)/shard_map/ppermute | solution.py:23
  246.5 5.6 %collective-permute-start.37 = (f32[1,2,3,1,6,128]{5,4,3,2,1,0:T(8,128)S(1)}, f32[1,2,3,1,6,128]{5,4,3,2,1,0:T(8,128)S(1)}, u32[]{:S(2)}, u32[]{:S(2)}) collective-permute-start(f32[1,2,3,1,6,128]{5,4,3,2,1,0:T(8,128)S(1)} %get-tuple-element.585), channel_id=1, source_target_pairs={{0,1},{1,2},{2,3},{3,0},{4,5},{5,6},{6,7},{7,4},{8,9},{9,10},{10,1... | collective-permute-start | bytes 55304 | tf_op jit(solution)/shard_map/ppermute | solution.py:23
  258.6 5.6 %collective-permute-start.41 = (f32[1,2,3,1,6,128]{5,4,3,2,1,0:T(8,128)S(1)}, f32[1,2,3,1,6,128]{5,4,3,2,1,0:T(8,128)S(1)}, u32[]{:S(2)}, u32[]{:S(2)}) collective-permute-start(f32[1,2,3,1,6,128]{5,4,3,2,1,0:T(8,128)S(1)} %get-tuple-element.581), channel_id=1, source_target_pairs={{0,1},{1,2},{2,3},{3,0},{4,5},{5,6},{6,7},{7,4},{8,9},{9,10},{10,1... | collective-permute-start | bytes 55304 | tf_op jit(solution)/shard_map/ppermute | solution.py:23
  302.1 4.1 collective-permute-start.44
  303.4 5.9 %collective-permute-start.45 = (f32[1,2,3,1,6,128]{5,4,3,2,1,0:T(8,128)S(1)}, f32[1,2,3,1,6,128]{5,4,3,2,1,0:T(8,128)S(1)}, u32[]{:S(2)}, u32[]{:S(2)}) collective-permute-start(f32[1,2,3,1,6,128]{5,4,3,2,1,0:T(8,128)S(1)} %get-tuple-element.577), channel_id=1, source_target_pairs={{0,1},{1,2},{2,3},{3,0},{4,5},{5,6},{6,7},{7,4},{8,9},{9,10},{10,1... | collective-permute-start | bytes 55304 | tf_op jit(solution)/shard_map/ppermute | solution.py:23
  314.9 4.1 collective-permute-start.48
  315.5 5.9 %collective-permute-start.49 = (f32[1,2,3,1,6,128]{5,4,3,2,1,0:T(8,128)S(1)}, f32[1,2,3,1,6,128]{5,4,3,2,1,0:T(8,128)S(1)}, u32[]{:S(2)}, u32[]{:S(2)}) collective-permute-start(f32[1,2,3,1,6,128]{5,4,3,2,1,0:T(8,128)S(1)} %get-tuple-element.573), channel_id=1, source_target_pairs={{0,1},{1,2},{2,3},{3,0},{4,5},{5,6},{6,7},{7,4},{8,9},{9,10},{10,1... | collective-permute-start | bytes 55304 | tf_op jit(solution)/shard_map/ppermute | solution.py:23
  360.6 5.6 %collective-permute-start.53 = (f32[1,2,3,1,6,128]{5,4,3,2,1,0:T(8,128)S(1)}, f32[1,2,3,1,6,128]{5,4,3,2,1,0:T(8,128)S(1)}, u32[]{:S(2)}, u32[]{:S(2)}) collective-permute-start(f32[1,2,3,1,6,128]{5,4,3,2,1,0:T(8,128)S(1)} %get-tuple-element.569), channel_id=1, source_target_pairs={{0,1},{1,2},{2,3},{3,0},{4,5},{5,6},{6,7},{7,4},{8,9},{9,10},{10,1... | collective-permute-start | bytes 55304 | tf_op jit(solution)/shard_map/ppermute | solution.py:23
  372.7 5.6 %collective-permute-start.57 = (f32[1,2,3,1,6,128]{5,4,3,2,1,0:T(8,128)S(1)}, f32[1,2,3,1,6,128]{5,4,3,2,1,0:T(8,128)S(1)}, u32[]{:S(2)}, u32[]{:S(2)}) collective-permute-start(f32[1,2,3,1,6,128]{5,4,3,2,1,0:T(8,128)S(1)} %get-tuple-element.565), channel_id=1, source_target_pairs={{0,1},{1,2},{2,3},{3,0},{4,5},{5,6},{6,7},{7,4},{8,9},{9,10},{10,1... | collective-permute-start | bytes 55304 | tf_op jit(solution)/shard_map/ppermute | solution.py:23
  417.4 5.9 %collective-permute-start.61 = (f32[1,2,3,1,6,128]{5,4,3,2,1,0:T(8,128)S(1)}, f32[1,2,3,1,6,128]{5,4,3,2,1,0:T(8,128)S(1)}, u32[]{:S(2)}, u32[]{:S(2)}) collective-permute-start(f32[1,2,3,1,6,128]{5,4,3,2,1,0:T(8,128)S(1)} %get-tuple-element.559), channel_id=1, source_target_pairs={{0,1},{1,2},{2,3},{3,0},{4,5},{5,6},{6,7},{7,4},{8,9},{9,10},{10,1... | collective-permute-start | bytes 55304 | tf_op jit(solution)/shard_map/ppermute | solution.py:23
  428.8 4.1 collective-permute-start.64
  429.4 5.9 %collective-permute-start.65 = (f32[1,2,3,1,6,128]{5,4,3,2,1,0:T(8,128)S(1)}, f32[1,2,3,1,6,128]{5,4,3,2,1,0:T(8,128)S(1)}, u32[]{:S(2)}, u32[]{:S(2)}) collective-permute-start(f32[1,2,3,1,6,128]{5,4,3,2,1,0:T(8,128)S(1)} %get-tuple-element.555), channel_id=1, source_target_pairs={{0,1},{1,2},{2,3},{3,0},{4,5},{5,6},{6,7},{7,4},{8,9},{9,10},{10,1... | collective-permute-start | bytes 55304 | tf_op jit(solution)/shard_map/ppermute | solution.py:23
  (46 other events, 264.9 us)
where the time goes:
time: 513 us; the launch traced here: 512 us
  blocking collectives  293 us (57%)
  waiting for transfers between devices  89.2 us (17%)
  starting transfers between devices  64.4 us (13%)
  local copies, waits for them, and re-layouts  22.3 us (4%)
  between operations  22 us (4%)
  other arithmetic  21.7 us (4%)
    psum x7, blocking collectives, on_device(): lax.psum((local_dot(direction, image), local_dot(residual, image), local_...  214 us
    ppermute x32, waiting for transfers between devices, extended(): lax.ppermute(lax.slice_in_dim(block, block.shape[dim] - width, None, axis...  59.6 us
    ppermute x32, starting transfers between devices, extended(): lax.ppermute(lax.slice_in_dim(block, 0, width, axis=dim), axis, backward)  41.5 us
    psum x1, blocking collectives, on_device(): total = lax.psum(jnp.sum(source * rational), ('grp', 'zt', 'xy'))  40.5 us
    psum x1, blocking collectives, on_device(): norm_now = lax.psum(local_dot(source, source), ('zt', 'xy'))  30.7 us
    ppermute x32, waiting for transfers between devices, extended(): lax.ppermute(lax.slice_in_dim(block, 0, width, axis=dim), axis, backward)  29.6 us
    ppermute x32, starting transfers between devices, extended(): lax.ppermute(lax.slice_in_dim(block, block.shape[dim] - width, None, axis...  21 us
  transfers between devices with their start and end apart: 66, of which 47 were waited for; matrix products, arithmetic and copies ran while one was open for 1% of the time, Pallas kernels for 0%

commit v1 on v0

--- a/solution.py
+++ b/solution.py
@@ -132,7 +132,7 @@
     direction = source
     solutions = jnp.zeros((shifts.shape[0],) + source.shape, jnp.float32)
     directions = jnp.broadcast_to(source[None], solutions.shape)
-    norm_now = lax.psum(local_dot(source, source), ("zt", "xy"))
+    norm_now = lax.psum(lax.psum(local_dot(source, source), "zt"), "xy")
     zeta_now = jnp.ones((shifts.shape[0], members), jnp.float32)
     zeta_old = jnp.ones((shifts.shape[0], members), jnp.float32)
     alpha_old = jnp.ones((members,), jnp.float32)

time: 513 us -> 529 us (1.031)
  blocking collectives: 293 us -> 310 us
    psum x7 -> x8, blocking collectives: 214 us -> 245 us  [on_device(): lax.psum((local_dot(direction, image), local_dot(residual, image), local_...]
    psum x1 -> x2, blocking collectives: 30.7 us -> 16.4 us  [on_device(): norm_now = lax.psum(lax.psum(local_dot(source, source), 'zt'), 'xy')]
where the time goes in v1:
time: 529 us; the launch traced here: 528 us
  blocking collectives  310 us (59%)
  waiting for transfers between devices  87.7 us (17%)
  starting transfers between devices  64.3 us (12%)
  local copies, waits for them, and re-layouts  22.3 us (4%)
  between operations  21.8 us (4%)
  other arithmetic  21.7 us (4%)
    psum x8, blocking collectives, on_device(): lax.psum((local_dot(direction, image), local_dot(residual, image), local_...  245 us
    ppermute x32, waiting for transfers between devices, extended(): lax.ppermute(lax.slice_in_dim(block, block.shape[dim] - width, None, axis...  58.4 us
    psum x1, blocking collectives, on_device(): total = lax.psum(jnp.sum(source * rational), ('grp', 'zt', 'xy'))  40.9 us
    ppermute x32, starting transfers between devices, extended(): lax.ppermute(lax.slice_in_dim(block, 0, width, axis=dim), axis, backward)  40.3 us
    ppermute x32, waiting for transfers between devices, extended(): lax.ppermute(lax.slice_in_dim(block, 0, width, axis=dim), axis, backward)  29.3 us
    ppermute x32, starting transfers between devices, extended(): lax.ppermute(lax.slice_in_dim(block, block.shape[dim] - width, None, axis...  22.2 us
    psum x2, blocking collectives, on_device(): norm_now = lax.psum(lax.psum(local_dot(source, source), 'zt'), 'xy')  16.4 us
  transfers between devices with their start and end apart: 66, of which 47 were waited for; matrix products, arithmetic and copies ran while one was open for 1% of the time, Pallas kernels for 0%

profile of v1, /device:TPU:0, one launch (start us, length us, event | category | flops | bytes accessed | tf_op | source)
XLA Modules:
  0.0 528.2 jit_solution(12589498465614910364)
XLA Ops:
  0.7 7.8 %all_gather.3 = f32[4,2,3,3,2,4,128]{6,5,4,3,2,1,0:T(4,128)S(1)} all-gather(f32[2,2,3,3,2,4,128]{6,5,4,3,2,1,0:T(4,128)} %param.10), channel_id=1, replica_groups=mesh['grp'=2,'zt'=4,'xy'=4] {'grp'}, dimensions={0}, use_global_device_ids=true | all-gather | bytes 442368 | tf_op jit(solution)/shard_map/all_gather | solution.py:112
  18.0 3.9 collective-permute-done.5
  31.7 2.6 collective-permute-done.9
  36.1 6.5 %psum.171 = f32[1]{0:T(128)} all-reduce(f32[1]{0:T(128)} %bitcast), channel_id=1, replica_groups=mesh['grp'=2,'zt'=4,'xy'=4] {'zt'}, use_global_device_ids=true, to_apply=%region_1.2 | all-reduce | flops 1 | bytes 8 | tf_op jit(solution)/shard_map/psum | solution.py:135
  42.6 10.0 %psum.172 = f32[1]{0:T(128)} all-reduce(f32[1]{0:T(128)} %psum.171), channel_id=1, replica_groups=mesh['grp'=2,'zt'=4,'xy'=4] {'xy'}, use_global_device_ids=true, to_apply=%region_2.3 | all-reduce | flops 1 | bytes 8 | tf_op jit(solution)/shard_map/psum | solution.py:135
  52.6 31.3 %all-reduce.7 = (f32[1]{0:T(128)}, f32[1]{0:T(128)}) all-reduce(f32[1]{0:T(128)} %bitcast.76, f32[1]{0:T(128)} %bitcast.80), channel_id=1, replica_groups=mesh['grp'=2,'zt'=4,'xy'=4] {'zt','xy'}, use_global_device_ids=true, to_apply=%region_36.37 | all-reduce | flops 2 | bytes 16 | tf_op jit(solution)/shard_map/psum | solution.py:143
  110.8 30.8 %all-reduce.6 = (f32[1]{0:T(128)}, f32[1]{0:T(128)}, f32[1]{0:T(128)}) all-reduce(f32[1]{0:T(128)} %bitcast.140, f32[1]{0:T(128)} %bitcast.144, f32[1]{0:T(128)} %bitcast.145), channel_id=1, replica_groups=mesh['grp'=2,'zt'=4,'xy'=4] {'zt','xy'}, use_global_device_ids=true, to_apply=%region_72.73 | all-reduce | flops 3 | bytes 24 | tf_op jit(solution)/shard_map/psum | solution.py:143
  151.1 2.9 collective-permute-done.21
  163.7 2.4 collective-permute-done.25
  167.9 30.8 %all-reduce.5 = (f32[1]{0:T(128)}, f32[1]{0:T(128)}, f32[1]{0:T(128)}) all-reduce(f32[1]{0:T(128)} %bitcast.205, f32[1]{0:T(128)} %bitcast.209, f32[1]{0:T(128)} %bitcast.210), channel_id=1, replica_groups=mesh['grp'=2,'zt'=4,'xy'=4] {'zt','xy'}, use_global_device_ids=true, to_apply=%region_110.111 | all-reduce | flops 3 | bytes 24 | tf_op jit(solution)/shard_map/psum | solution.py:143
  208.3 2.8 collective-permute-done.29
  220.7 2.5 collective-permute-done.33
  225.0 30.4 %all-reduce.4 = (f32[1]{0:T(128)}, f32[1]{0:T(128)}, f32[1]{0:T(128)}) all-reduce(f32[1]{0:T(128)} %bitcast.270, f32[1]{0:T(128)} %bitcast.274, f32[1]{0:T(128)} %bitcast.275), channel_id=1, replica_groups=mesh['grp'=2,'zt'=4,'xy'=4] {'zt','xy'}, use_global_device_ids=true, to_apply=%region_148.149 | all-reduce | flops 3 | bytes 24 | tf_op jit(solution)/shard_map/psum | solution.py:143
  265.1 3.1 collective-permute-done.37
  282.0 30.6 %all-reduce.3 = (f32[1]{0:T(128)}, f32[1]{0:T(128)}, f32[1]{0:T(128)}) all-reduce(f32[1]{0:T(128)} %bitcast.335, f32[1]{0:T(128)} %bitcast.339, f32[1]{0:T(128)} %bitcast.340), channel_id=1, replica_groups=mesh['grp'=2,'zt'=4,'xy'=4] {'zt','xy'}, use_global_device_ids=true, to_apply=%region_186.187 | all-reduce | flops 3 | bytes 24 | tf_op jit(solution)/shard_map/psum | solution.py:143
  322.3 2.8 collective-permute-done.45
  334.6 2.5 collective-permute-done.49
  339.0 30.4 %all-reduce.2 = (f32[1]{0:T(128)}, f32[1]{0:T(128)}, f32[1]{0:T(128)}) all-reduce(f32[1]{0:T(128)} %bitcast.400, f32[1]{0:T(128)} %bitcast.404, f32[1]{0:T(128)} %bitcast.405), channel_id=1, replica_groups=mesh['grp'=2,'zt'=4,'xy'=4] {'zt','xy'}, use_global_device_ids=true, to_apply=%region_224.225 | all-reduce | flops 3 | bytes 24 | tf_op jit(solution)/shard_map/psum | solution.py:143
  379.2 3.1 collective-permute-done.53
  396.1 30.6 %all-reduce.1 = (f32[1]{0:T(128)}, f32[1]{0:T(128)}, f32[1]{0:T(128)}) all-reduce(f32[1]{0:T(128)} %bitcast.465, f32[1]{0:T(128)} %bitcast.469, f32[1]{0:T(128)} %bitcast.470), channel_id=1, replica_groups=mesh['grp'=2,'zt'=4,'xy'=4] {'zt','xy'}, use_global_device_ids=true, to_apply=%region_262.263 | all-reduce | flops 3 | bytes 24 | tf_op jit(solution)/shard_map/psum | solution.py:143
  436.3 2.8 collective-permute-done.61
  448.6 2.5 collective-permute-done.65
  452.8 30.3 %psum.193 = f32[1]{0:T(128)} all-reduce(f32[1]{0:T(128)} %bitcast.531), channel_id=1, replica_groups=mesh['grp'=2,'zt'=4,'xy'=4] {'zt','xy'}, use_global_device_ids=true, to_apply=%region_300.301 | all-reduce | flops 1 | bytes 8 | tf_op jit(solution)/shard_map/psum | solution.py:143
  485.5 40.9 %psum.194 = f32[]{:T(128)} all-reduce(f32[]{:T(128)} %multiply_reduce_fusion.1), channel_id=1, replica_groups=mesh['grp'=2,'zt'=4,'xy'=4] {'grp','zt','xy'}, use_global_device_ids=true, to_apply=%region_303.304 | all-reduce | flops 1 | bytes 8 | tf_op jit(solution)/shard_map/psum | solution.py:172
  (741 shorter events, 162.1 us)
Async XLA Ops:
  8.8 13.1 %collective-permute-start = (f32[2,3,3,1,4,128]{5,4,3,2,1,0:T(4,128)S(1)}, f32[2,3,3,1,4,128]{5,4,3,2,1,0:T(4,128)S(1)}, u32[]{:S(2)}, u32[]{:S(2)}) collective-permute-start(f32[2,3,3,1,4,128]{5,4,3,2,1,0:T(4,128)S(1)} %slice.3115), channel_id=1, source_target_pairs={{3,0},{0,1},{1,2},{2,3},{7,4},{4,5},{5,6},{6,7},{11,8},{8,9},{9,10... | collective-permute-start | bytes 110600 | tf_op jit(solution)/shard_map/ppermute | solution.py:14
  10.7 11.4 %collective-permute-start.1 = (f32[2,3,3,2,1,128]{5,4,3,2,1,0:T(1,128)S(1)}, f32[2,3,3,2,1,128]{5,4,3,2,1,0:T(1,128)S(1)}, u32[]{:S(2)}, u32[]{:S(2)}) collective-permute-start(f32[2,3,3,2,1,128]{5,4,3,2,1,0:T(1,128)S(1)} %slice.3117), channel_id=1, source_target_pairs={{12,0},{0,4},{4,8},{8,12},{13,1},{1,5},{5,9},{9,13},{14,2},{2,6},{... | collective-permute-start | bytes 55304 | tf_op jit(solution)/shard_map/ppermute | solution.py:14
  16.2 5.6 %collective-permute-start.5 = (f32[1,2,3,1,6,128]{5,4,3,2,1,0:T(8,128)S(1)}, f32[1,2,3,1,6,128]{5,4,3,2,1,0:T(8,128)S(1)}, u32[]{:S(2)}, u32[]{:S(2)}) collective-permute-start(f32[1,2,3,1,6,128]{5,4,3,2,1,0:T(8,128)S(1)} %get-tuple-element.616), channel_id=1, source_target_pairs={{0,1},{1,2},{2,3},{3,0},{4,5},{5,6},{6,7},{7,4},{8,9},{9,10},{10,1... | collective-permute-start | bytes 55304 | tf_op jit(solution)/shard_map/ppermute | solution.py:23
  28.6 5.8 %collective-permute-start.9 = (f32[1,2,3,1,6,128]{5,4,3,2,1,0:T(8,128)S(1)}, f32[1,2,3,1,6,128]{5,4,3,2,1,0:T(8,128)S(1)}, u32[]{:S(2)}, u32[]{:S(2)}) collective-permute-start(f32[1,2,3,1,6,128]{5,4,3,2,1,0:T(8,128)S(1)} %get-tuple-element.612), channel_id=1, source_target_pairs={{0,1},{1,2},{2,3},{3,0},{4,5},{5,6},{6,7},{7,4},{8,9},{9,10},{10,1... | collective-permute-start | bytes 55304 | tf_op jit(solution)/shard_map/ppermute | solution.py:23
  91.7 5.6 %collective-permute-start.13 = (f32[1,2,3,1,6,128]{5,4,3,2,1,0:T(8,128)S(1)}, f32[1,2,3,1,6,128]{5,4,3,2,1,0:T(8,128)S(1)}, u32[]{:S(2)}, u32[]{:S(2)}) collective-permute-start(f32[1,2,3,1,6,128]{5,4,3,2,1,0:T(8,128)S(1)} %get-tuple-element.608), channel_id=1, source_target_pairs={{0,1},{1,2},{2,3},{3,0},{4,5},{5,6},{6,7},{7,4},{8,9},{9,10},{10,1... | collective-permute-start | bytes 55304 | tf_op jit(solution)/shard_map/ppermute | solution.py:23
  103.4 5.6 %collective-permute-start.17 = (f32[1,2,3,1,6,128]{5,4,3,2,1,0:T(8,128)S(1)}, f32[1,2,3,1,6,128]{5,4,3,2,1,0:T(8,128)S(1)}, u32[]{:S(2)}, u32[]{:S(2)}) collective-permute-start(f32[1,2,3,1,6,128]{5,4,3,2,1,0:T(8,128)S(1)} %get-tuple-element.604), channel_id=1, source_target_pairs={{0,1},{1,2},{2,3},{3,0},{4,5},{5,6},{6,7},{7,4},{8,9},{9,10},{10,1... | collective-permute-start | bytes 55304 | tf_op jit(solution)/shard_map/ppermute | solution.py:23
  148.2 5.8 %collective-permute-start.21 = (f32[1,2,3,1,6,128]{5,4,3,2,1,0:T(8,128)S(1)}, f32[1,2,3,1,6,128]{5,4,3,2,1,0:T(8,128)S(1)}, u32[]{:S(2)}, u32[]{:S(2)}) collective-permute-start(f32[1,2,3,1,6,128]{5,4,3,2,1,0:T(8,128)S(1)} %get-tuple-element.600), channel_id=1, source_target_pairs={{0,1},{1,2},{2,3},{3,0},{4,5},{5,6},{6,7},{7,4},{8,9},{9,10},{10,1... | collective-permute-start | bytes 55304 | tf_op jit(solution)/shard_map/ppermute | solution.py:23
  159.6 4.1 collective-permute-start.24
  160.3 5.8 %collective-permute-start.25 = (f32[1,2,3,1,6,128]{5,4,3,2,1,0:T(8,128)S(1)}, f32[1,2,3,1,6,128]{5,4,3,2,1,0:T(8,128)S(1)}, u32[]{:S(2)}, u32[]{:S(2)}) collective-permute-start(f32[1,2,3,1,6,128]{5,4,3,2,1,0:T(8,128)S(1)} %get-tuple-element.596), channel_id=1, source_target_pairs={{0,1},{1,2},{2,3},{3,0},{4,5},{5,6},{6,7},{7,4},{8,9},{9,10},{10,1... | collective-permute-start | bytes 55304 | tf_op jit(solution)/shard_map/ppermute | solution.py:23
  205.5 5.6 %collective-permute-start.29 = (f32[1,2,3,1,6,128]{5,4,3,2,1,0:T(8,128)S(1)}, f32[1,2,3,1,6,128]{5,4,3,2,1,0:T(8,128)S(1)}, u32[]{:S(2)}, u32[]{:S(2)}) collective-permute-start(f32[1,2,3,1,6,128]{5,4,3,2,1,0:T(8,128)S(1)} %get-tuple-element.592), channel_id=1, source_target_pairs={{0,1},{1,2},{2,3},{3,0},{4,5},{5,6},{6,7},{7,4},{8,9},{9,10},{10,1... | collective-permute-start | bytes 55304 | tf_op jit(solution)/shard_map/ppermute | solution.py:23
  216.8 3.9 collective-permute-start.32
  217.6 5.6 %collective-permute-start.33 = (f32[1,2,3,1,6,128]{5,4,3,2,1,0:T(8,128)S(1)}, f32[1,2,3,1,6,128]{5,4,3,2,1,0:T(8,128)S(1)}, u32[]{:S(2)}, u32[]{:S(2)}) collective-permute-start(f32[1,2,3,1,6,128]{5,4,3,2,1,0:T(8,128)S(1)} %get-tuple-element.588), channel_id=1, source_target_pairs={{0,1},{1,2},{2,3},{3,0},{4,5},{5,6},{6,7},{7,4},{8,9},{9,10},{10,1... | collective-permute-start | bytes 55304 | tf_op jit(solution)/shard_map/ppermute | solution.py:23
  261.1 4.1 collective-permute-start.36
  262.3 5.8 %collective-permute-start.37 = (f32[1,2,3,1,6,128]{5,4,3,2,1,0:T(8,128)S(1)}, f32[1,2,3,1,6,128]{5,4,3,2,1,0:T(8,128)S(1)}, u32[]{:S(2)}, u32[]{:S(2)}) collective-permute-start(f32[1,2,3,1,6,128]{5,4,3,2,1,0:T(8,128)S(1)} %get-tuple-element.584), channel_id=1, source_target_pairs={{0,1},{1,2},{2,3},{3,0},{4,5},{5,6},{6,7},{7,4},{8,9},{9,10},{10,1... | collective-permute-start | bytes 55304 | tf_op jit(solution)/shard_map/ppermute | solution.py:23
  273.8 4.1 collective-permute-start.40
  274.4 5.9 %collective-permute-start.41 = (f32[1,2,3,1,6,128]{5,4,3,2,1,0:T(8,128)S(1)}, f32[1,2,3,1,6,128]{5,4,3,2,1,0:T(8,128)S(1)}, u32[]{:S(2)}, u32[]{:S(2)}) collective-permute-start(f32[1,2,3,1,6,128]{5,4,3,2,1,0:T(8,128)S(1)} %get-tuple-element.580), channel_id=1, source_target_pairs={{0,1},{1,2},{2,3},{3,0},{4,5},{5,6},{6,7},{7,4},{8,9},{9,10},{10,1... | collective-permute-start | bytes 55304 | tf_op jit(solution)/shard_map/ppermute | solution.py:23
  319.5 5.6 %collective-permute-start.45 = (f32[1,2,3,1,6,128]{5,4,3,2,1,0:T(8,128)S(1)}, f32[1,2,3,1,6,128]{5,4,3,2,1,0:T(8,128)S(1)}, u32[]{:S(2)}, u32[]{:S(2)}) collective-permute-start(f32[1,2,3,1,6,128]{5,4,3,2,1,0:T(8,128)S(1)} %get-tuple-element.576), channel_id=1, source_target_pairs={{0,1},{1,2},{2,3},{3,0},{4,5},{5,6},{6,7},{7,4},{8,9},{9,10},{10,1... | collective-permute-start | bytes 55304 | tf_op jit(solution)/shard_map/ppermute | solution.py:23
  331.6 5.6 %collective-permute-start.49 = (f32[1,2,3,1,6,128]{5,4,3,2,1,0:T(8,128)S(1)}, f32[1,2,3,1,6,128]{5,4,3,2,1,0:T(8,128)S(1)}, u32[]{:S(2)}, u32[]{:S(2)}) collective-permute-start(f32[1,2,3,1,6,128]{5,4,3,2,1,0:T(8,128)S(1)} %get-tuple-element.572), channel_id=1, source_target_pairs={{0,1},{1,2},{2,3},{3,0},{4,5},{5,6},{6,7},{7,4},{8,9},{9,10},{10,1... | collective-permute-start | bytes 55304 | tf_op jit(solution)/shard_map/ppermute | solution.py:23
  375.1 4.1 collective-permute-start.52
  376.4 5.8 %collective-permute-start.53 = (f32[1,2,3,1,6,128]{5,4,3,2,1,0:T(8,128)S(1)}, f32[1,2,3,1,6,128]{5,4,3,2,1,0:T(8,128)S(1)}, u32[]{:S(2)}, u32[]{:S(2)}) collective-permute-start(f32[1,2,3,1,6,128]{5,4,3,2,1,0:T(8,128)S(1)} %get-tuple-element.568), channel_id=1, source_target_pairs={{0,1},{1,2},{2,3},{3,0},{4,5},{5,6},{6,7},{7,4},{8,9},{9,10},{10,1... | collective-permute-start | bytes 55304 | tf_op jit(solution)/shard_map/ppermute | solution.py:23
  387.9 4.1 collective-permute-start.56
  388.5 5.9 %collective-permute-start.57 = (f32[1,2,3,1,6,128]{5,4,3,2,1,0:T(8,128)S(1)}, f32[1,2,3,1,6,128]{5,4,3,2,1,0:T(8,128)S(1)}, u32[]{:S(2)}, u32[]{:S(2)}) collective-permute-start(f32[1,2,3,1,6,128]{5,4,3,2,1,0:T(8,128)S(1)} %get-tuple-element.564), channel_id=1, source_target_pairs={{0,1},{1,2},{2,3},{3,0},{4,5},{5,6},{6,7},{7,4},{8,9},{9,10},{10,1... | collective-permute-start | bytes 55304 | tf_op jit(solution)/shard_map/ppermute | solution.py:23
  433.5 5.6 %collective-permute-start.61 = (f32[1,2,3,1,6,128]{5,4,3,2,1,0:T(8,128)S(1)}, f32[1,2,3,1,6,128]{5,4,3,2,1,0:T(8,128)S(1)}, u32[]{:S(2)}, u32[]{:S(2)}) collective-permute-start(f32[1,2,3,1,6,128]{5,4,3,2,1,0:T(8,128)S(1)} %get-tuple-element.558), channel_id=1, source_target_pairs={{0,1},{1,2},{2,3},{3,0},{4,5},{5,6},{6,7},{7,4},{8,9},{9,10},{10,1... | collective-permute-start | bytes 55304 | tf_op jit(solution)/shard_map/ppermute | solution.py:23
  445.5 5.6 %collective-permute-start.65 = (f32[1,2,3,1,6,128]{5,4,3,2,1,0:T(8,128)S(1)}, f32[1,2,3,1,6,128]{5,4,3,2,1,0:T(8,128)S(1)}, u32[]{:S(2)}, u32[]{:S(2)}) collective-permute-start(f32[1,2,3,1,6,128]{5,4,3,2,1,0:T(8,128)S(1)} %get-tuple-element.554), channel_id=1, source_target_pairs={{0,1},{1,2},{2,3},{3,0},{4,5},{5,6},{6,7},{7,4},{8,9},{9,10},{10,1... | collective-permute-start | bytes 55304 | tf_op jit(solution)/shard_map/ppermute | solution.py:23
  (46 other events, 264.8 us)
